TPU v7x, 32 devices: a whole 2x2x4 slice. The times are simulated.
32 devices in a mesh: node: 16 (over z, y, core), ell: 2 (over x).
Axes of the slice: x: 2, y: 2, z: 4, core: 2. Of those that a mesh axis runs over, the one named last changes fastest.
Arguments:
- table_zero: bfloat16 [6144, 1536], P('node', 'ell'), may hold values from -1 to 1
- table_two: bfloat16 [6144, 1536], P('node', 'ell'), may hold values from -1 to 1
- spectrum: bfloat16 [1536], P('ell'), may hold values from -0.15625 to 0.15625
- weights: float32 [6144], P('node'), may hold values from 0.02551552 to 0.25515518
Outputs:
- kernel: float32 [1536, 1536], P('node', 'ell')
All inputs are finite; a program needn't handle non-finite values.
Results may differ from a plain program's by a relative error of at most 0.0029.
Values may be sent and summed in bfloat16 or wider, within the bound.
A program may use at most 128 MiB of HBM per device.

v0:
```python
import jax
import jax.numpy as jnp
from jax import lax
from jax.sharding import PartitionSpec as P


def contract_nodes(left, right):
    return lax.dot_general(
        left, right, (((0,), (0,)), ((), ())), preferred_element_type=jnp.float32
    )


def per_device(table_zero, table_two, spectrum, weights):
    partial_value = jnp.dot(table_zero, spectrum, preferred_element_type=jnp.float32)
    xi = lax.psum(partial_value, "ell")
    gathered = lax.all_gather(table_zero, "ell", axis=1, tiled=True)
    weighted = ((weights * xi)[:, None] * gathered.astype(jnp.float32)).astype(jnp.bfloat16)
    return lax.psum_scatter(
        contract_nodes(weighted, table_two), "node", scatter_dimension=0, tiled=True
    )


def solution(mesh):
    placed = (P("node", "ell"), P("node", "ell"), P("ell"), P("node"))
    return jax.shard_map(
        per_device, mesh=mesh, in_specs=placed, out_specs=P("node", "ell"), check_vma=False
    )
```

profile of v0, /device:TPU:0, one launch (start us, length us, event | category | flops | bytes accessed | tf_op | source)
XLA Modules:
  0.0 121.9 jit_solution(10760141810804105223)
XLA Ops:
  6.5 0.0 copy-start
  6.5 0.0 all-gather.2.cloned.1.call-start
  6.5 0.7 all-gather.2.cloned.1.call-update
  7.3 0.0 reduce-scatter.2.cloned.1.call-start
  7.3 0.7 reshape.1
  8.0 1.4 %convolution_reduce_fusion = f32[384]{0:T(512)S(1)} fusion(bf16[384,768]{1,0:T(8,128)(2,1)} %param.4, bf16[768,1]{0,1:T(2,128)(2,1)S(1)} %reshape.1), kind=kOutput, calls=%fused_computation.3 | convolution fusion | flops 589824 | bytes 592896 | tf_op jit(solution)/shard_map/dot_general | solution.py:14
  9.3 5.8 %psum.7 = f32[384]{0:T(512)S(1)} all-reduce(f32[384]{0:T(512)S(1)} %convolution_reduce_fusion), channel_id=1, replica_groups=mesh['node'=16,'ell'=2] {'ell'}, use_global_device_ids=true, to_apply=%region_0.0 | all-reduce | flops 384 | bytes 3072 | tf_op jit(solution)/shard_map/psum | solution.py:15
  15.2 0.7 mul.11
  15.9 18.5 %all-gather.2.cloned.1.call-done = bf16[384,1536]{1,0:T(8,128)(2,1)} async-done(((bf16[384,768]{1,0:T(8,128)(2,1)}), bf16[384,1536]{1,0:T(8,128)(2,1)}) %all-gather.2.cloned.1.call-update) | async-done | bytes 1179664 | tf_op jit(solution)/shard_map/all_gather | solution.py:16
  34.4 0.0 copy-done
  34.4 4.9 %fusion = f32[1536,768]{1,0:T(8,128)} fusion(bf16[384,768]{1,0:T(8,128)(2,1)S(1)} %copy-done, bf16[384,1536]{1,0:T(8,128)(2,1)} %all-gather.2.cloned.1.call-done, f32[384]{0:T(512)S(1)} %mul.11), kind=kOutput, calls=%fused_computation.1 | convolution fusion | flops 907739136 | bytes 6489600 | tf_op jit(solution)/shard_map/dot_general | solution.py:8
  39.3 0.0 reduce-scatter.2.cloned.1.call-update
  39.3 75.7 %reduce-scatter.2.cloned.1.call-done = f32[96,768]{1,0:T(8,128)} async-done(((f32[1536,768]{1,0:T(8,128)}), f32[96,768]{1,0:T(8,128)}) %reduce-scatter.2.cloned.1.call-update) | async-done | bytes 294928 | tf_op jit(solution)/shard_map/reduce_scatter | solution.py:18
Async XLA Ops:
  6.5 27.9 %copy-start = (bf16[384,768]{1,0:T(8,128)(2,1)S(1)}, bf16[384,768]{1,0:T(8,128)(2,1)}, u32[]{:S(2)}) copy-start(bf16[384,768]{1,0:T(8,128)(2,1)} %param.5) | copy-start | bytes 1769476
  6.5 27.8 %all-gather.2.cloned.1.call-start = ((), (), s32[]{:S(2)}) async-start(), calls=%async_computation.1 | async-start | bytes 1769472 | tf_op jit(solution)/shard_map/all_gather | solution.py:16
  7.3 107.8 %reduce-scatter.2.cloned.1.call-start = ((), (), s32[]{:S(2)}) async-start(), calls=%async_computation.2 | async-start | bytes 5013504 | tf_op jit(solution)/shard_map/reduce_scatter | solution.py:18
Sparse Core Ops, SparseCore 0:
  8.9 25.4 all-gather.1
  39.4 75.5 reduce-scatter.1
where the time goes:
time: 122 us
  waiting for transfers between devices  94.9 us (78%)
  between operations  13.4 us (11%)
  matrix products  6.26 us (5%)
  blocking collectives  5.85 us (5%)
    reduce_scatter x1, waiting for transfers between devices, per_device(): lax.psum_scatter(contract_nodes(weighted, table_two), 'node', scatter_dim...  75.7 us
    all_gather x1, waiting for transfers between devices, per_device(): gathered = lax.all_gather(table_zero, 'ell', axis=1, tiled=True)  18.5 us
    psum x1, blocking collectives, per_device(): xi = lax.psum(partial_value, 'ell')  5.85 us
    dot_general x1, matrix products, contract_nodes(): lax.dot_general(left, right, (((0,), (0,)), ((), ())), preferred_element_...  4.9 us
  transfers between devices with their start and end apart: 2, of which 2 were waited for; matrix products, arithmetic and copies ran while one was open for 2% of the time, Pallas kernels for 0%

commit v1 on v0

--- a/solution.py
+++ b/solution.py
@@ -2,6 +2,12 @@
 import jax.numpy as jnp
 from jax import lax
 from jax.sharding import PartitionSpec as P
+
+
+def gather_blocks(shard, name, dim):
+    parts = lax.all_gather(shard, name, axis=0, tiled=False)
+    result = jnp.concatenate(parts, axis=dim)
+    return result
 
 
 def contract_nodes(left, right):
@@ -13,7 +19,7 @@
 def per_device(table_zero, table_two, spectrum, weights):
     partial_value = jnp.dot(table_zero, spectrum, preferred_element_type=jnp.float32)
     xi = lax.psum(partial_value, "ell")
-    gathered = lax.all_gather(table_zero, "ell", axis=1, tiled=True)
+    gathered = gather_blocks(table_zero, "ell", 1)
     weighted = ((weights * xi)[:, None] * gathered.astype(jnp.float32)).astype(jnp.bfloat16)
     return lax.psum_scatter(
         contract_nodes(weighted, table_two), "node", scatter_dimension=0, tiled=True

time: 122 us -> 126 us (1.033)
  other arithmetic: 0.68 us -> 3.73 us
  local copies, waits for them, and re-layouts: 0.69 us -> 2.72 us
  matrix products: 6.26 us -> 4.87 us
    convert_element_type x0 -> x2, other arithmetic: none -> 3.04 us  [the longest x1 2.85 us: per_device(): gathered.astype(jnp.float32)]
    convert_element_type x0 -> x1, local copies, waits for them, and re-layouts: none -> 2.03 us  [per_device(): gathered.astype(jnp.float32)]
    dot_general x1, matrix products: 4.9 us -> 3.52 us  [contract_nodes(): lax.dot_general(left, right, (((0,), (0,)), ((), ())), preferred_element_...]
where the time goes in v1:
time: 126 us
  waiting for transfers between devices  94.9 us (75%)
  between operations  13.4 us (11%)
  blocking collectives  5.85 us (5%)
  matrix products  4.87 us (4%)
  other arithmetic  3.73 us (3%)
  local copies, waits for them, and re-layouts  2.72 us (2%)
    reduce_scatter x1, waiting for transfers between devices, per_device(): lax.psum_scatter(contract_nodes(weighted, table_two), 'node', scatter_dim...  75.7 us
    all_gather x1, waiting for transfers between devices, gather_blocks(): parts = lax.all_gather(shard, name, axis=0, tiled=False)  18.5 us
    psum x1, blocking collectives, per_device(): xi = lax.psum(partial_value, 'ell')  5.85 us
    dot_general x1, matrix products, contract_nodes(): lax.dot_general(left, right, (((0,), (0,)), ((), ())), preferred_element_...  3.52 us
    convert_element_type x1, other arithmetic, per_device(): gathered.astype(jnp.float32)  2.85 us
  transfers between devices with their start and end apart: 2, of which 2 were waited for; matrix products, arithmetic and copies ran while one was open for 2% of the time, Pallas kernels for 0%

profile of v1, /device:TPU:0, one launch (start us, length us, event | category | flops | bytes accessed | tf_op | source)
XLA Modules:
  0.0 125.6 jit_solution(16815173560662781296)
XLA Ops:
  6.5 0.0 copy-start
  6.5 0.0 all-gather.3.cloned.1.call-start
  6.5 0.7 all-gather.3.cloned.1.call-update
  7.3 0.0 reduce-scatter.2.cloned.1.call-start
  7.3 0.7 reshape.8
  8.0 1.4 %convolution_reduce_fusion = f32[384]{0:T(512)S(1)} fusion(bf16[384,768]{1,0:T(8,128)(2,1)} %param.4, bf16[768,1]{0,1:T(2,128)(2,1)S(1)} %reshape.8), kind=kOutput, calls=%fused_computation.3 | convolution fusion | flops 589824 | bytes 592896 | tf_op jit(solution)/shard_map/dot_general | solution.py:20
  9.3 5.8 %psum.7 = f32[384]{0:T(512)S(1)} all-reduce(f32[384]{0:T(512)S(1)} %convolution_reduce_fusion), channel_id=1, replica_groups=mesh['node'=16,'ell'=2] {'ell'}, use_global_device_ids=true, to_apply=%region_0.0 | all-reduce | flops 384 | bytes 3072 | tf_op jit(solution)/shard_map/psum | solution.py:21
  15.2 0.7 mul.11
  15.9 18.5 %all-gather.3.cloned.1.call-done = bf16[768,768]{1,0:T(8,128)(2,1)} async-done(((bf16[384,768]{1,0:T(8,128)(2,1)}), bf16[768,768]{1,0:T(8,128)(2,1)}) %all-gather.3.cloned.1.call-update) | async-done | bytes 1179664 | tf_op jit(solution)/shard_map/all_gather | solution.py:8
  34.4 2.9 %convert_bitcast_fusion = f32[384,2,768]{2,0,1:T(8,128)} fusion(bf16[2,384,768]{2,1,0:T(8,128)(2,1)} %bitcast.12), kind=kLoop, calls=%fused_computation | loop fusion | flops 589824 | bytes 3538944 | tf_op jit(solution)/shard_map/convert_element_type | solution.py:23
  37.2 2.0 %copy.5 = f32[384,2,768]{0,2,1:T(8,128)S(1)} copy(f32[384,2,768]{2,0,1:T(8,128)} %convert_bitcast_fusion) | data formatting | bytes 4718592 | tf_op jit(solution)/shard_map/convert_element_type | solution.py:23
  39.3 0.2 fusion
  39.5 0.0 copy-done
  39.5 3.5 %fusion.1 = f32[1536,768]{1,0:T(8,128)} fusion(bf16[384,1536]{0,1:T(8,128)(2,1)S(1)} %fusion, bf16[384,768]{1,0:T(8,128)(2,1)S(1)} %copy-done), kind=kOutput, calls=%fused_computation.4 | convolution fusion | flops 905969664 | bytes 6488064 | tf_op jit(solution)/shard_map/dot_general | solution.py:14
  43.0 0.0 reduce-scatter.2.cloned.1.call-update
  43.0 75.7 %reduce-scatter.2.cloned.1.call-done = f32[96,768]{1,0:T(8,128)} async-done(((f32[1536,768]{1,0:T(8,128)}), f32[96,768]{1,0:T(8,128)}) %reduce-scatter.2.cloned.1.call-update) | async-done | bytes 294928 | tf_op jit(solution)/shard_map/reduce_scatter | solution.py:24
Async XLA Ops:
  6.5 32.9 %copy-start = (bf16[384,768]{1,0:T(8,128)(2,1)S(1)}, bf16[384,768]{1,0:T(8,128)(2,1)}, u32[]{:S(2)}) copy-start(bf16[384,768]{1,0:T(8,128)(2,1)} %param.5) | copy-start | bytes 1769476
  6.5 27.8 %all-gather.3.cloned.1.call-start = ((), (), s32[]{:S(2)}) async-start(), calls=%async_computation.2 | async-start | bytes 1769472 | tf_op jit(solution)/shard_map/all_gather | solution.py:8
  7.3 111.5 %reduce-scatter.2.cloned.1.call-start = ((), (), s32[]{:S(2)}) async-start(), calls=%async_computation.1 | async-start | bytes 5013504 | tf_op jit(solution)/shard_map/reduce_scatter | solution.py:24
Sparse Core Ops, SparseCore 0:
  8.9 25.4 all-gather.2
  43.1 75.5 reduce-scatter.1
